TPU v7x, 32 devices: a whole 2x2x4 slice. The times are simulated.
32 devices in a mesh: zero: 16 (over z, y, core), width: 2 (over x).
Axes of the slice: x: 2, y: 2, z: 4, core: 2. Of those that a mesh axis runs over, the one named last changes fastest.
Arguments:
- slopes_in: float32 [128, 128, 4096], P(None, 'zero', 'width'), may hold values from -6 to 6
- moments_in: float32 [128, 128, 4096], P(None, 'zero', 'width'), may hold values from -6 to 6
- weights_in: float32 [128, 128, 4096], P(None, 'zero', 'width'), may hold values from -0.1875 to 0.1875
Outputs:
- new_weights: float32 [128, 128, 4096], P(None, 'zero', 'width')
- new_momentum: float32 [128, 128, 4096], P(None, 'zero', 'width')
All inputs are finite; a program needn't handle non-finite values.
Results may differ from a plain program's by a relative error of at most 0.0001.
Values sent between devices are 32-bit elements; how exact they have to be, the bound alone decides.
A program may use at most 128 MiB of HBM per device.

v0:
```python
import functools

import jax
import jax.numpy as jnp
from jax import lax
from jax.experimental import pallas as pl
from jax.experimental.pallas import tpu as pltpu
from jax.sharding import PartitionSpec as P

ITERS = 3
MESH = pl.DeviceIdType.MESH

hold_rate = 0.8
learn_rate = 0.8
decay_rate = 0.1


def dot(a, b):
    return jnp.dot(a, b, precision=lax.Precision.HIGHEST, preferred_element_type=jnp.float32)


def kernel(
    nz, nw, sent, weights, new_weights, held, made, back, old, gram, heard,
    fwd_send, fwd_recv, gram_send, gram_recv, ret_send, ret_recv, old_sem, new_sem,
):
    me = lax.axis_index("zero")
    side = lax.axis_index("width")
    mats, rows, cols = sent.shape
    mine = mats // nz
    total_rows = nz * rows

    barrier = pltpu.get_barrier_semaphore()

    def greet_zero(k, c):
        pl.semaphore_signal(barrier, inc=1, device_id=(lax.rem(me + k, nz), side), device_id_type=MESH)
        return c

    def greet_width(k, c):
        pl.semaphore_signal(barrier, inc=1, device_id=(me, lax.rem(side + k, nw)), device_id_type=MESH)
        return c

    lax.fori_loop(1, nz, greet_zero, 0)
    lax.fori_loop(1, nw, greet_width, 0)
    pl.semaphore_wait(barrier, nz - 1 + nw - 1)

    def forward(j, c):
        pltpu.make_async_copy(sent.at[me * mine + j], held.at[j, me], fwd_recv.at[j]).start()

        def one(k, c):
            to = lax.rem(me + k, nz)
            pltpu.make_async_remote_copy(
                src_ref=sent.at[to * mine + j],
                dst_ref=held.at[j, me],
                send_sem=fwd_send,
                recv_sem=fwd_recv.at[j],
                device_id=(to, side),
                device_id_type=MESH,
            ).start()
            return c

        return lax.fori_loop(1, nz, one, c)

    lax.fori_loop(0, mine, forward, 0)
    pltpu.make_async_copy(weights, old, old_sem).start()

    def gram_of(j):
        pltpu.make_async_copy(held.at[j], held.at[j], fwd_recv.at[j]).wait()
        x = held[j].reshape(total_rows, cols)
        gram[j] = lax.dot_general(
            x, x, (((1,), (1,)), ((), ())),
            precision=lax.Precision.HIGHEST, preferred_element_type=jnp.float32,
        )

        def one(k, c):
            to = lax.rem(side + k, nw)
            pltpu.make_async_remote_copy(
                src_ref=gram.at[j],
                dst_ref=heard.at[j, k - 1],
                send_sem=gram_send,
                recv_sem=gram_recv.at[j],
                device_id=(me, to),
                device_id_type=MESH,
            ).start()
            return c

        lax.fori_loop(1, nw, one, 0)

    def finish(j):
        pltpu.make_async_copy(heard.at[j], heard.at[j], gram_recv.at[j]).wait()
        full = gram[j] + jnp.sum(heard[j], axis=0)
        at_diag = lax.broadcasted_iota(jnp.int32, full.shape, 0) == lax.broadcasted_iota(jnp.int32, full.shape, 1)
        squares = jnp.sum(jnp.sum(jnp.where(at_diag, full, 0.0), axis=1, keepdims=True), axis=0, keepdims=True)
        scale = lax.rsqrt(squares + 1e-06)
        a = full * scale * scale
        eye = jnp.where(at_diag, 3.4445, 0.0)
        mix = None
        for step in range(ITERS):
            m = eye - 4.775 * a + 2.0315 * dot(a, a)
            if step < ITERS - 1:
                a = dot(dot(m, a), m)
            mix = m if mix is None else dot(m, mix)
        mix = mix * scale
        y = dot(mix, held[j].reshape(total_rows, cols))
        made[j] = y.reshape(nz, rows, cols)

        def one(k, c):
            to = lax.rem(me + k, nz)
            pltpu.make_async_remote_copy(
                src_ref=made.at[j, to],
                dst_ref=back.at[me * mine + j],
                send_sem=ret_send,
                recv_sem=ret_recv.at[j],
                device_id=(to, side),
                device_id_type=MESH,
            ).start()
            return c

        lax.fori_loop(1, nz, one, 0)
        back[me * mine + j] = made[j, me]

    gram_of(0)

    def stage(j, c):
        gram_of(j)
        finish(j - 1)
        return c

    lax.fori_loop(1, mine, stage, 0)
    finish(mine - 1)

    pltpu.make_async_copy(weights, old, old_sem).wait()

    def update(j, c):
        came = back.at[pl.ds(0, nz - 1)]
        pltpu.make_async_copy(came, came, ret_recv.at[j]).wait()

        def one(k, c):
            at = k * mine + j
            back[at] = (1.0 - learn_rate * decay_rate) * old[at] - learn_rate * back[at]
            return c

        def leave(k, c):
            at = k * mine + j
            pltpu.make_async_copy(back.at[at], new_weights.at[at], new_sem).start()
            return c

        lax.fori_loop(0, nz, one, 0)
        return lax.fori_loop(0, nz, leave, c)

    lax.fori_loop(0, mine, update, 0)

    others = pl.ds(0, (nz - 1) * mine)
    pltpu.make_async_copy(sent.at[others], sent.at[others], fwd_send).wait()
    pltpu.make_async_copy(heard, heard, gram_send).wait()
    pltpu.make_async_copy(back.at[others], back.at[others], ret_send).wait()
    pltpu.make_async_copy(back, new_weights, new_sem).wait()


def stepped(nz, nw, direction, weights):
    mats, rows, cols = direction.shape
    mine = mats // nz
    n = nz * rows
    return pl.pallas_call(
        functools.partial(kernel, nz, nw),
        out_shape=jax.ShapeDtypeStruct(direction.shape, jnp.float32),
        in_specs=[pl.BlockSpec(memory_space=pl.ANY), pl.BlockSpec(memory_space=pltpu.HBM)],
        out_specs=pl.BlockSpec(memory_space=pltpu.HBM),
        scratch_shapes=[
            pltpu.VMEM((mine, nz, rows, cols), jnp.float32),
            pltpu.VMEM((mine, nz, rows, cols), jnp.float32),
            pltpu.VMEM(direction.shape, jnp.float32),
            pltpu.VMEM(direction.shape, jnp.float32),
            pltpu.VMEM((mine, n, n), jnp.float32),
            pltpu.VMEM((mine, nw - 1, n, n), jnp.float32),
            pltpu.SemaphoreType.DMA,
            pltpu.SemaphoreType.DMA((mine,)),
            pltpu.SemaphoreType.DMA,
            pltpu.SemaphoreType.DMA((mine,)),
            pltpu.SemaphoreType.DMA,
            pltpu.SemaphoreType.DMA((mine,)),
            pltpu.SemaphoreType.DMA,
            pltpu.SemaphoreType.DMA,
        ],
        compiler_params=pltpu.CompilerParams(
            collective_id=0, has_side_effects=True, vmem_limit_bytes=38 * 1024 * 1024
        ),
        name="stepped",
    )(direction, weights)


def body(nz, nw, slopes_in, moments_in, weights_in):
    new_momentum = hold_rate * moments_in + slopes_in
    direction = hold_rate * new_momentum + slopes_in
    new_weights = stepped(nz, nw, direction, weights_in)
    return (new_weights, new_momentum)


def solution(mesh):
    spec = P(None, "zero", "width")
    run = functools.partial(body, mesh.shape["zero"], mesh.shape["width"])
    return jax.shard_map(run, mesh=mesh, in_specs=(spec,) * 3, out_specs=(spec,) * 2, check_vma=False)
```

profile of v0, /device:TPU:15, one launch (start us, length us, event | category | flops | bytes accessed | tf_op | source)
XLA Modules:
  0.0 383.7 jit_solution(9001984215896335340)
XLA Ops:
  0.6 11.3 %multiply_add_fusion = (f32[128,8,2048]{2,1,0:T(8,128)}, f32[128,8,2048]{2,1,0:T(8,128)}) fusion(f32[128,8,2048]{2,1,0:T(8,128)} %param.3, f32[128,8,2048]{2,1,0:T(8,128)} %param.4), kind=kLoop, calls=%fused_computation | loop fusion | flops 8388608 | bytes 33554432 | tf_op jit(solution)/shard_map/add | solution.py:193
  11.9 368.3 %stepped.1 = f32[128,8,2048]{2,1,0:T(8,128)S(1)} custom-call(f32[128,8,2048]{2,1,0:T(8,128)} %get-tuple-element.2.sent, f32[128,8,2048]{2,1,0:T(8,128)} %weights.1), custom_call_target="tpu_custom_call" | custom-call | tf_op jit(solution)/shard_map/stepped/pallas_call | solution.py:163
  380.3 3.4 copy.6
where the time goes:
time: 384 us
  Pallas kernels  368 us (96%)
  other arithmetic  11.3 us (3%)
    pallas_call x1, Pallas kernels, stepped(): pl.pallas_call(functools.partial(kernel, nz, nw), out_shape=jax.ShapeDtyp...  368 us
    add x1, other arithmetic, body(): direction = hold_rate * new_momentum + slopes_in  11.3 us

commit v1 on v0

v1 whole, which is shorter than its diff:
```python
import functools

import jax
import jax.numpy as jnp
from jax import lax
from jax.experimental import pallas as pl
from jax.experimental.pallas import tpu as pltpu
from jax.sharding import PartitionSpec as P

ITERS = 3
MESH = pl.DeviceIdType.MESH

hold_rate = 0.8
learn_rate = 0.8
decay_rate = 0.1


def dot(a, b):
    return jnp.dot(a, b, precision=lax.Precision.HIGHEST, preferred_element_type=jnp.float32)


def kernel(
    nz, nw, slopes, moments, weights, res, mom, sent, held, made, back, gram, heard,
    slope_sem, moment_sem, weight_sem, fwd_send, fwd_recv, own_sem, gram_send, gram_recv, ret_send, ret_recv,
):
    me = lax.axis_index("zero")
    side = lax.axis_index("width")
    _, mine, rows, cols = sent.shape
    total_rows = nz * rows
    half = nz // 2
    my_half = me // half

    def far(k):
        return (1 - my_half) * half + lax.rem(me + k, half)

    def near(k):
        return my_half * half + lax.rem(me + k, half)

    barrier = pltpu.get_barrier_semaphore()

    def greet_zero(k, c):
        pl.semaphore_signal(barrier, inc=1, device_id=(lax.rem(me + k, nz), side), device_id_type=MESH)
        return c

    def greet_width(k, c):
        pl.semaphore_signal(barrier, inc=1, device_id=(me, lax.rem(side + k, nw)), device_id_type=MESH)
        return c

    lax.fori_loop(1, nz, greet_zero, 0)
    lax.fori_loop(1, nw, greet_width, 0)

    def load(j, c):
        pltpu.make_async_copy(slopes.at[:, j], sent.at[:, j], slope_sem.at[j]).start()
        pltpu.make_async_copy(moments.at[:, j], mom.at[:, j], moment_sem.at[j]).start()
        return c

    lax.fori_loop(0, mine, load, 0)

    def direction(j):
        pltpu.make_async_copy(slopes.at[:, j], sent.at[:, j], slope_sem.at[j]).wait()
        pltpu.make_async_copy(moments.at[:, j], mom.at[:, j], moment_sem.at[j]).wait()

        def one(k, c):
            slope = sent[k, j]
            fresh = hold_rate * mom[k, j] + slope
            mom[k, j] = fresh
            sent[k, j] = hold_rate * fresh + slope
            return c

        lax.fori_loop(0, nz, one, 0)

    def send(j, to):
        pltpu.make_async_remote_copy(
            src_ref=sent.at[to, j],
            dst_ref=held.at[j, me],
            send_sem=fwd_send,
            recv_sem=fwd_recv.at[j],
            device_id=(to, side),
            device_id_type=MESH,
        ).start()

    def forward(j):
        def far_one(k, c):
            send(j, far(k))
            return c

        def near_one(k, c):
            send(j, near(k))
            return c

        lax.fori_loop(0, half, far_one, 0)
        lax.fori_loop(1, half, near_one, 0)
        pltpu.make_async_copy(sent.at[me, j], held.at[j, me], own_sem.at[j]).start()

    direction(0)
    pl.semaphore_wait(barrier, nz - 1 + nw - 1)

    def ahead(j, c):
        forward(j - 1)
        direction(j)
        return c

    lax.fori_loop(1, mine, ahead, 0)
    forward(mine - 1)
    pltpu.make_async_copy(weights, res, weight_sem).start()

    def gram_of(j):
        others = held.at[j, pl.ds(0, nz - 1)]
        pltpu.make_async_copy(others, others, fwd_recv.at[j]).wait()
        pltpu.make_async_copy(sent.at[me, j], held.at[j, me], own_sem.at[j]).wait()
        x = held[j].reshape(total_rows, cols)
        gram[j] = lax.dot_general(
            x, x, (((1,), (1,)), ((), ())),
            precision=lax.Precision.HIGHEST, preferred_element_type=jnp.float32,
        )

        def one(k, c):
            to = lax.rem(side + k, nw)
            pltpu.make_async_remote_copy(
                src_ref=gram.at[j],
                dst_ref=heard.at[j, k - 1],
                send_sem=gram_send,
                recv_sem=gram_recv.at[j],
                device_id=(me, to),
                device_id_type=MESH,
            ).start()
            return c

        lax.fori_loop(1, nw, one, 0)

    def give(j, to):
        pltpu.make_async_remote_copy(
            src_ref=made.at[j, to],
            dst_ref=back.at[me, j],
            send_sem=ret_send,
            recv_sem=ret_recv.at[j],
            device_id=(to, side),
            device_id_type=MESH,
        ).start()

    def finish(j):
        pltpu.make_async_copy(heard.at[j], heard.at[j], gram_recv.at[j]).wait()
        full = gram[j] + jnp.sum(heard[j], axis=0)
        at_diag = lax.broadcasted_iota(jnp.int32, full.shape, 0) == lax.broadcasted_iota(jnp.int32, full.shape, 1)
        squares = jnp.sum(jnp.sum(jnp.where(at_diag, full, 0.0), axis=1, keepdims=True), axis=0, keepdims=True)
        scale = lax.rsqrt(squares + 1e-06)
        a = full * scale * scale
        eye = jnp.where(at_diag, 3.4445, 0.0)
        mix = None
        for step in range(ITERS):
            m = eye - 4.775 * a + 2.0315 * dot(a, a)
            if step < ITERS - 1:
                a = dot(dot(m, a), m)
            mix = m if mix is None else dot(m, mix)
        mix = mix * scale
        y = dot(mix, held[j].reshape(total_rows, cols))
        made[j] = y.reshape(nz, rows, cols)

        def far_one(k, c):
            give(j, far(k))
            return c

        def near_one(k, c):
            give(j, near(k))
            return c

        lax.fori_loop(0, half, far_one, 0)
        lax.fori_loop(1, half, near_one, 0)
        back[me, j] = made[j, me]

    gram_of(0)

    def stage(j, c):
        gram_of(j)
        finish(j - 1)
        return c

    lax.fori_loop(1, mine, stage, 0)
    finish(mine - 1)

    pltpu.make_async_copy(weights, res, weight_sem).wait()

    def update(j, c):
        came = back.at[pl.ds(0, nz - 1), j]
        pltpu.make_async_copy(came, came, ret_recv.at[j]).wait()

        def one(k, c):
            res[k, j] = (1.0 - learn_rate * decay_rate) * res[k, j] - learn_rate * back[k, j]
            return c

        return lax.fori_loop(0, nz, one, c)

    lax.fori_loop(0, mine, update, 0)

    others = sent.at[pl.ds(0, nz - 1)]
    pltpu.make_async_copy(others, others, fwd_send).wait()
    pltpu.make_async_copy(heard, heard, gram_send).wait()
    pltpu.make_async_copy(others, others, ret_send).wait()


def stepped(nz, nw, slopes, moments, weights):
    mats, rows, cols = slopes.shape
    mine = mats // nz
    n = nz * rows
    split = (nz, mine, rows, cols)
    hbm = pl.BlockSpec(memory_space=pltpu.HBM)
    buffer = pltpu.VMEM(split, jnp.float32)
    gathered = pltpu.VMEM((mine, nz, rows, cols), jnp.float32)
    each = pltpu.SemaphoreType.DMA((mine,))
    once = pltpu.SemaphoreType.DMA
    out, mom = pl.pallas_call(
        functools.partial(kernel, nz, nw),
        out_shape=(pltpu.VMEM(split, jnp.float32),) * 2,
        in_specs=[hbm] * 3,
        out_specs=[pl.BlockSpec(memory_space=pltpu.VMEM)] * 2,
        scratch_shapes=[
            buffer,
            gathered,
            gathered,
            buffer,
            pltpu.VMEM((mine, n, n), jnp.float32),
            pltpu.VMEM((mine, nw - 1, n, n), jnp.float32),
            each,
            each,
            once,
            once,
            each,
            each,
            once,
            each,
            once,
            each,
        ],
        compiler_params=pltpu.CompilerParams(
            collective_id=0, has_side_effects=True, vmem_limit_bytes=35 * 1024 * 1024
        ),
        name="stepped",
    )(slopes.reshape(split), moments.reshape(split), weights.reshape(split))
    return out.reshape(slopes.shape), mom.reshape(slopes.shape)


def body(nz, nw, slopes_in, moments_in, weights_in):
    return stepped(nz, nw, slopes_in, moments_in, weights_in)


def solution(mesh):
    spec = P(None, "zero", "width")
    run = functools.partial(body, mesh.shape["zero"], mesh.shape["width"])
    return jax.shard_map(run, mesh=mesh, in_specs=(spec,) * 3, out_specs=(spec,) * 2, check_vma=False)
```

time: 384 us -> 376 us (0.979)
  other arithmetic: 11.3 us -> 0 us
    add x1 -> x0, other arithmetic: 11.3 us -> none  [body(): direction = hold_rate * new_momentum + slopes_in]
where the time goes in v1:
time: 376 us; the launch traced here: 373 us
  Pallas kernels  366 us (97%)
  local copies, waits for them, and re-layouts  6.8 us (2%)
    pallas_call x1, Pallas kernels, stepped(): pl.pallas_call(functools.partial(kernel, nz, nw), out_shape=(pltpu.VMEM(s...  366 us

profile of v1, /device:TPU:15, one launch (start us, length us, event | category | flops | bytes accessed | tf_op | source)
XLA Modules:
  0.0 373.4 jit_solution(1190054083087420409)
XLA Ops:
  0.6 365.9 %stepped.1 = (f32[16,8,8,2048]{3,2,1,0:T(8,128)S(1)}, f32[16,8,8,2048]{3,2,1,0:T(8,128)S(1)}) custom-call(f32[16,8,8,2048]{3,2,1,0:T(8,128)} %bitcast.7, f32[16,8,8,2048]{3,2,1,0:T(8,128)} %bitcast.8, f32[16,8,8,2048]{3,2,1,0:T(8,128)} %bitcast.9), custom_call_target="tpu_custom_call" | custom-call | tf_op jit(solution)/shard_map/stepped/pallas_call | solution.py:211
  366.6 3.4 copy.7
  370.0 3.4 copy.8

commit v2 on v1

--- a/solution.py
+++ b/solution.py
@@ -28,10 +28,12 @@
     _, mine, rows, cols = sent.shape
     total_rows = nz * rows
     half = nz // 2
+    quarter = nz // 4
     my_half = me // half
 
     def far(k):
-        return (1 - my_half) * half + lax.rem(me + k, half)
+        outer = 1 - k // quarter
+        return (1 - my_half) * (half + outer * quarter) + my_half * (1 - outer) * quarter + lax.rem(me + k, quarter)
 
     def near(k):
         return my_half * half + lax.rem(me + k, half)
@@ -54,7 +56,7 @@
         pltpu.make_async_copy(moments.at[:, j], mom.at[:, j], moment_sem.at[j]).start()
         return c
 
-    lax.fori_loop(0, mine, load, 0)
+    load(0, 0)
 
     def direction(j):
         pltpu.make_async_copy(slopes.at[:, j], sent.at[:, j], slope_sem.at[j]).wait()
@@ -93,6 +95,7 @@
         pltpu.make_async_copy(sent.at[me, j], held.at[j, me], own_sem.at[j]).start()
 
     direction(0)
+    lax.fori_loop(1, mine, load, 0)
     pl.semaphore_wait(barrier, nz - 1 + nw - 1)
 
     def ahead(j, c):
@@ -196,6 +199,27 @@
     pltpu.make_async_copy(others, others, fwd_send).wait()
     pltpu.make_async_copy(heard, heard, gram_send).wait()
     pltpu.make_async_copy(others, others, ret_send).wait()
+
+
+def leave(res, mom, new_weights, new_momentum, sems):
+    def copies(k):
+        return (
+            pltpu.make_async_copy(res.at[k], new_weights.at[k], sems.at[0, k]),
+            pltpu.make_async_copy(mom.at[k], new_momentum.at[k], sems.at[1, k]),
+        )
+
+    def go(k, c):
+        for copy in copies(k):
+            copy.start()
+        return c
+
+    def end(k, c):
+        for copy in copies(k):
+            copy.wait()
+        return c
+
+    lax.fori_loop(0, res.shape[0], go, 0)
+    lax.fori_loop(0, res.shape[0], end, 0)
 
 
 def stepped(nz, nw, slopes, moments, weights):
@@ -236,6 +260,15 @@
         ),
         name="stepped",
     )(slopes.reshape(split), moments.reshape(split), weights.reshape(split))
+    out, mom = pl.pallas_call(
+        leave,
+        out_shape=(jax.ShapeDtypeStruct(split, jnp.float32),) * 2,
+        in_specs=[pl.BlockSpec(memory_space=pltpu.VMEM)] * 2,
+        out_specs=[hbm] * 2,
+        scratch_shapes=[pltpu.SemaphoreType.DMA((2, nz))],
+        compiler_params=pltpu.CompilerParams(vmem_limit_bytes=1024 * 1024),
+        name="leave",
+    )(out, mom)
     return out.reshape(slopes.shape), mom.reshape(slopes.shape)
 
 

time: 376 us -> 373 us (level)
  local copies, waits for them, and re-layouts: 6.8 us -> 0 us
  Pallas kernels: 366 us -> 372 us
    unnamed x2 -> x0, local copies, waits for them, and re-layouts: 6.8 us -> none
    pallas_call x0 -> x1, Pallas kernels: none -> 6.08 us  [stepped(): pl.pallas_call(leave, out_shape=(jax.ShapeDtypeStruct(split, jnp.float32)...]
where the time goes in v2:
time: 373 us
  Pallas kernels  372 us (100%)
    pallas_call x1, Pallas kernels, stepped(): pl.pallas_call(functools.partial(kernel, nz, nw), out_shape=(pltpu.VMEM(s...  366 us

profile of v2, /device:TPU:15, one launch (start us, length us, event | category | flops | bytes accessed | tf_op | source)
XLA Modules:
  0.0 372.8 jit_solution(9816091574576867070)
XLA Ops:
  0.6 366.1 %stepped.1 = (f32[16,8,8,2048]{3,2,1,0:T(8,128)S(1)}, f32[16,8,8,2048]{3,2,1,0:T(8,128)S(1)}) custom-call(f32[16,8,8,2048]{3,2,1,0:T(8,128)} %bitcast.5, f32[16,8,8,2048]{3,2,1,0:T(8,128)} %bitcast.6, f32[16,8,8,2048]{3,2,1,0:T(8,128)} %bitcast.7), custom_call_target="tpu_custom_call" | custom-call | tf_op jit(solution)/shard_map/stepped/pallas_call | solution.py:235
  366.7 6.1 %leave.1 = (f32[16,8,8,2048]{3,2,1,0:T(8,128)}, f32[16,8,8,2048]{3,2,1,0:T(8,128)}) custom-call(f32[16,8,8,2048]{3,2,1,0:T(8,128)S(1)} %get-tuple-element.6.res, f32[16,8,8,2048]{3,2,1,0:T(8,128)S(1)} %get-tuple-element.7.mom), custom_call_target="tpu_custom_call" | custom-call | tf_op jit(solution)/shard_map/leave/pallas_call | solution.py:263

commit v3 on v2

--- a/solution.py
+++ b/solution.py
@@ -30,6 +30,9 @@
     half = nz // 2
     quarter = nz // 4
     my_half = me // half
+    my_quarter = me // quarter
+    inner = jnp.logical_and(my_quarter >= 1, my_quarter <= 2)
+    partner = my_half * quarter + (1 - my_half) * half + lax.rem(me, quarter)
 
     def far(k):
         outer = 1 - k // quarter
@@ -40,36 +43,54 @@
 
     barrier = pltpu.get_barrier_semaphore()
 
-    def greet_zero(k, c):
-        pl.semaphore_signal(barrier, inc=1, device_id=(lax.rem(me + k, nz), side), device_id_type=MESH)
-        return c
-
-    def greet_width(k, c):
-        pl.semaphore_signal(barrier, inc=1, device_id=(me, lax.rem(side + k, nw)), device_id_type=MESH)
-        return c
-
-    lax.fori_loop(1, nz, greet_zero, 0)
-    lax.fori_loop(1, nw, greet_width, 0)
-
-    def load(j, c):
-        pltpu.make_async_copy(slopes.at[:, j], sent.at[:, j], slope_sem.at[j]).start()
-        pltpu.make_async_copy(moments.at[:, j], mom.at[:, j], moment_sem.at[j]).start()
-        return c
-
-    load(0, 0)
-
-    def direction(j):
-        pltpu.make_async_copy(slopes.at[:, j], sent.at[:, j], slope_sem.at[j]).wait()
-        pltpu.make_async_copy(moments.at[:, j], mom.at[:, j], moment_sem.at[j]).wait()
-
-        def one(k, c):
+    def greet(to, across):
+        pl.semaphore_signal(barrier, inc=1, device_id=(to, lax.rem(side + across, nw)), device_id_type=MESH)
+
+    def inner_of(k):
+        return quarter + lax.rem(me + quarter + k, half)
+
+    def outer_of(k):
+        return lax.rem(half + quarter + lax.rem(me + quarter + k, half), nz)
+
+    @pl.when(inner)
+    def _():
+        greet(partner, 0)
+
+    @pl.when(jnp.logical_not(inner))
+    def _():
+        def greet_outer(k, c):
+            greet(outer_of(k), 0)
+            return c
+
+        def greet_across(k, c):
+            greet(me, k)
+            return c
+
+        lax.fori_loop(1, half, greet_outer, 0)
+        lax.fori_loop(1, nw, greet_across, 0)
+
+    def slope_copy(k):
+        return pltpu.make_async_copy(slopes.at[k], sent.at[k], slope_sem.at[k])
+
+    def moment_copy(k):
+        return pltpu.make_async_copy(moments.at[k], mom.at[k], moment_sem.at[k])
+
+    def load(k):
+        slope_copy(k).start()
+        moment_copy(k).start()
+
+    def direction(k):
+        slope_copy(k).wait()
+        moment_copy(k).wait()
+
+        def one(j, c):
             slope = sent[k, j]
             fresh = hold_rate * mom[k, j] + slope
             mom[k, j] = fresh
             sent[k, j] = hold_rate * fresh + slope
             return c
 
-        lax.fori_loop(0, nz, one, 0)
+        lax.fori_loop(0, mine, one, 0)
 
     def send(j, to):
         pltpu.make_async_remote_copy(
@@ -81,7 +102,58 @@
             device_id_type=MESH,
         ).start()
 
-    def forward(j):
+    def other(k):
+        return lax.rem(partner + k, nz)
+
+    load(partner)
+
+    def load_one(k, c):
+        load(other(k))
+        return c
+
+    def direction_one(k, c):
+        direction(other(k))
+        return c
+
+    direction(partner)
+    lax.fori_loop(1, nz, load_one, 0)
+
+    @pl.when(inner)
+    def _():
+        pl.semaphore_wait(barrier, 1)
+
+        def early(j, c):
+            send(j, partner)
+            return c
+
+        lax.fori_loop(0, mine, early, 0)
+
+        def greet_outer(k, c):
+            def one(across, c):
+                greet(outer_of(k), across)
+                return c
+
+            return lax.fori_loop(0, nw, one, c)
+
+        lax.fori_loop(0, half, greet_outer, 0)
+
+    lax.fori_loop(1, nz, direction_one, 0)
+
+    @pl.when(inner)
+    def _():
+        pl.semaphore_wait(barrier, half)
+
+    @pl.when(jnp.logical_not(inner))
+    def _():
+        pl.semaphore_wait(barrier, half - 1 + nw - 1 + half * nw)
+
+        def greet_inner(k, c):
+            greet(inner_of(k), 0)
+            return c
+
+        lax.fori_loop(0, half, greet_inner, 0)
+
+    def forward(j, c):
         def far_one(k, c):
             send(j, far(k))
             return c
@@ -90,21 +162,21 @@
             send(j, near(k))
             return c
 
-        lax.fori_loop(0, half, far_one, 0)
+        lax.fori_loop(0, quarter, far_one, 0)
+
+        @pl.when(inner)
+        def _():
+            lax.fori_loop(quarter + 1, half, far_one, 0)
+
+        @pl.when(jnp.logical_not(inner))
+        def _():
+            lax.fori_loop(quarter, half, far_one, 0)
+
         lax.fori_loop(1, half, near_one, 0)
         pltpu.make_async_copy(sent.at[me, j], held.at[j, me], own_sem.at[j]).start()
-
-    direction(0)
-    lax.fori_loop(1, mine, load, 0)
-    pl.semaphore_wait(barrier, nz - 1 + nw - 1)
-
-    def ahead(j, c):
-        forward(j - 1)
-        direction(j)
-        return c
-
-    lax.fori_loop(1, mine, ahead, 0)
-    forward(mine - 1)
+        return c
+
+    lax.fori_loop(0, mine, forward, 0)
     pltpu.make_async_copy(weights, res, weight_sem).start()
 
     def gram_of(j):
@@ -167,7 +239,12 @@
             give(j, near(k))
             return c
 
-        lax.fori_loop(0, half, far_one, 0)
+        def inner_one(k, c):
+            give(j, (1 - my_half) * half + my_half * quarter + k)
+            return c
+
+        lax.fori_loop(0, quarter, far_one, 0)
+        lax.fori_loop(0, quarter, inner_one, 0)
         lax.fori_loop(1, half, near_one, 0)
         back[me, j] = made[j, me]
 
@@ -244,8 +321,8 @@
             buffer,
             pltpu.VMEM((mine, n, n), jnp.float32),
             pltpu.VMEM((mine, nw - 1, n, n), jnp.float32),
-            each,
-            each,
+            pltpu.SemaphoreType.DMA((nz,)),
+            pltpu.SemaphoreType.DMA((nz,)),
             once,
             once,
             each,

time: 373 us -> 372 us (level)
  no operation moved by 1% of the time
where the time goes in v3:
time: 372 us
  Pallas kernels  371 us (100%)
    pallas_call x1, Pallas kernels, stepped(): pl.pallas_call(functools.partial(kernel, nz, nw), out_shape=(pltpu.VMEM(s...  365 us

profile of v3, /device:TPU:15, one launch (start us, length us, event | category | flops | bytes accessed | tf_op | source)
XLA Modules:
  0.0 371.8 jit_solution(5686591744856426113)
XLA Ops:
  0.6 365.1 %stepped.1 = (f32[16,8,8,2048]{3,2,1,0:T(8,128)S(1)}, f32[16,8,8,2048]{3,2,1,0:T(8,128)S(1)}) custom-call(f32[16,8,8,2048]{3,2,1,0:T(8,128)} %bitcast.5, f32[16,8,8,2048]{3,2,1,0:T(8,128)} %bitcast.6, f32[16,8,8,2048]{3,2,1,0:T(8,128)} %bitcast.7), custom_call_target="tpu_custom_call" | custom-call | tf_op jit(solution)/shard_map/stepped/pallas_call | solution.py:312
  365.7 6.1 %leave.1 = (f32[16,8,8,2048]{3,2,1,0:T(8,128)}, f32[16,8,8,2048]{3,2,1,0:T(8,128)}) custom-call(f32[16,8,8,2048]{3,2,1,0:T(8,128)S(1)} %get-tuple-element.6.res, f32[16,8,8,2048]{3,2,1,0:T(8,128)S(1)} %get-tuple-element.7.mom), custom_call_target="tpu_custom_call" | custom-call | tf_op jit(solution)/shard_map/leave/pallas_call | solution.py:340

commit v4 on v3

--- a/solution.py
+++ b/solution.py
@@ -115,8 +115,8 @@
         direction(other(k))
         return c
 
+    lax.fori_loop(1, nz, load_one, 0)
     direction(partner)
-    lax.fori_loop(1, nz, load_one, 0)
 
     @pl.when(inner)
     def _():
@@ -243,7 +243,11 @@
             give(j, (1 - my_half) * half + my_half * quarter + k)
             return c
 
-        lax.fori_loop(0, quarter, far_one, 0)
+        def outer_one(k, c):
+            give(j, (1 - my_half) * (half + quarter) + k)
+            return c
+
+        lax.fori_loop(0, quarter, outer_one, 0)
         lax.fori_loop(0, quarter, inner_one, 0)
         lax.fori_loop(1, half, near_one, 0)
         back[me, j] = made[j, me]
@@ -268,7 +272,7 @@
             res[k, j] = (1.0 - learn_rate * decay_rate) * res[k, j] - learn_rate * back[k, j]
             return c
 
-        return lax.fori_loop(0, nz, one, c)
+        return lax.fori_loop(0, nz, one, c, unroll=4)
 
     lax.fori_loop(0, mine, update, 0)
 

time: 372 us -> 372 us (level)
  no operation moved by 1% of the time
where the time goes in v4:
time: 372 us
  Pallas kernels  371 us (100%)
    pallas_call x1, Pallas kernels, stepped(): pl.pallas_call(functools.partial(kernel, nz, nw), out_shape=(pltpu.VMEM(s...  365 us

profile of v4, /device:TPU:15, one launch (start us, length us, event | category | flops | bytes accessed | tf_op | source)
XLA Modules:
  0.0 371.6 jit_solution(7772341592207385197)
XLA Ops:
  0.6 364.9 %stepped.1 = (f32[16,8,8,2048]{3,2,1,0:T(8,128)S(1)}, f32[16,8,8,2048]{3,2,1,0:T(8,128)S(1)}) custom-call(f32[16,8,8,2048]{3,2,1,0:T(8,128)} %bitcast.5, f32[16,8,8,2048]{3,2,1,0:T(8,128)} %bitcast.6, f32[16,8,8,2048]{3,2,1,0:T(8,128)} %bitcast.7), custom_call_target="tpu_custom_call" | custom-call | tf_op jit(solution)/shard_map/stepped/pallas_call | solution.py:316
  365.5 6.1 %leave.1 = (f32[16,8,8,2048]{3,2,1,0:T(8,128)}, f32[16,8,8,2048]{3,2,1,0:T(8,128)}) custom-call(f32[16,8,8,2048]{3,2,1,0:T(8,128)S(1)} %get-tuple-element.6.res, f32[16,8,8,2048]{3,2,1,0:T(8,128)S(1)} %get-tuple-element.7.mom), custom_call_target="tpu_custom_call" | custom-call | tf_op jit(solution)/shard_map/leave/pallas_call | solution.py:344

commit v5 on v4

--- a/solution.py
+++ b/solution.py
@@ -264,6 +264,10 @@
 
     pltpu.make_async_copy(weights, res, weight_sem).wait()
 
+    others = sent.at[pl.ds(0, nz - 1)]
+    pltpu.make_async_copy(others, others, fwd_send).wait()
+    pltpu.make_async_copy(heard, heard, gram_send).wait()
+
     def update(j, c):
         came = back.at[pl.ds(0, nz - 1), j]
         pltpu.make_async_copy(came, came, ret_recv.at[j]).wait()
@@ -272,13 +276,10 @@
             res[k, j] = (1.0 - learn_rate * decay_rate) * res[k, j] - learn_rate * back[k, j]
             return c
 
-        return lax.fori_loop(0, nz, one, c, unroll=4)
+        return lax.fori_loop(0, nz, one, c, unroll=8)
 
     lax.fori_loop(0, mine, update, 0)
 
-    others = sent.at[pl.ds(0, nz - 1)]
-    pltpu.make_async_copy(others, others, fwd_send).wait()
-    pltpu.make_async_copy(heard, heard, gram_send).wait()
     pltpu.make_async_copy(others, others, ret_send).wait()
 
 

time: 372 us -> 372 us (level)
  no operation moved by 1% of the time
where the time goes in v5:
time: 372 us
  Pallas kernels  371 us (100%)
    pallas_call x1, Pallas kernels, stepped(): pl.pallas_call(functools.partial(kernel, nz, nw), out_shape=(pltpu.VMEM(s...  365 us

profile of v5, /device:TPU:15, one launch (start us, length us, event | category | flops | bytes accessed | tf_op | source)
XLA Modules:
  0.0 371.6 jit_solution(14536271473703532731)
XLA Ops:
  0.6 364.9 %stepped.1 = (f32[16,8,8,2048]{3,2,1,0:T(8,128)S(1)}, f32[16,8,8,2048]{3,2,1,0:T(8,128)S(1)}) custom-call(f32[16,8,8,2048]{3,2,1,0:T(8,128)} %bitcast.5, f32[16,8,8,2048]{3,2,1,0:T(8,128)} %bitcast.6, f32[16,8,8,2048]{3,2,1,0:T(8,128)} %bitcast.7), custom_call_target="tpu_custom_call" | custom-call | tf_op jit(solution)/shard_map/stepped/pallas_call | solution.py:317
  365.5 6.1 %leave.1 = (f32[16,8,8,2048]{3,2,1,0:T(8,128)}, f32[16,8,8,2048]{3,2,1,0:T(8,128)}) custom-call(f32[16,8,8,2048]{3,2,1,0:T(8,128)S(1)} %get-tuple-element.6.res, f32[16,8,8,2048]{3,2,1,0:T(8,128)S(1)} %get-tuple-element.7.mom), custom_call_target="tpu_custom_call" | custom-call | tf_op jit(solution)/shard_map/leave/pallas_call | solution.py:345
